TPU v7x, 256 devices: a whole 4x4x8 slice. The times are simulated.
256 devices in a mesh: row: 4 (over y_lo, core), col: 64 (over z, y_hi, x).
Axes of the slice: x: 4, y: 4 (y_hi: 2, y_lo: 2; y = y_hi * 2 + y_lo), z: 8, core: 2. Of those that a mesh axis runs over, the one named last changes fastest.
Arguments:
- image: bfloat16 [8192, 1024], P(('col', 'row')), may hold values from -1 to 1
- text: bfloat16 [8192, 1024], P(('row', 'col')), may hold values from -1 to 1
- audio: bfloat16 [8192, 1024], P(('row', 'col')), may hold values from -1 to 1
Outputs:
- image_grad: float32 [8192, 1024], P(('col', 'row'))
- text_grad: float32 [8192, 1024], P(('row', 'col'))
- audio_grad: float32 [8192, 1024], P(('row', 'col'))
- loss: float32 [], replicated
All inputs are finite; a program needn't handle non-finite values.
Results may differ from a plain program's by a relative error of at most 0.0063.
Values may be sent and summed in bfloat16 or wider, within the bound.
No kernel may reach another device: no remote copies, remote signals or barrier semaphores. Data moves between devices by JAX's collectives and lax.ppermute only.
A program may use at most 64 MiB of HBM per device.

v0:
```python
import functools
import jax
import jax.numpy as jnp
from jax import lax
from jax.sharding import Mesh
from jax.sharding import PartitionSpec as P

ROW = ("row_0", "row_1")
COL = ("col_0", "col_1", "col_2")
ROW_COL = ("row_0", "row_1", "col_0", "col_1", "col_2")
COL_ROW = ("col_0", "col_1", "col_2", "row_0", "row_1")
logit_scale = 20.0
epsilon = 1e-06


def joined_along(parts, dim):
    lengths = list(parts.shape[1:])
    lengths[dim] *= parts.shape[0]
    return jnp.moveaxis(parts, 0, dim).reshape(lengths)


def stacked_from(array, axes, sequence):
    parts = array[None]
    for k in sequence:
        parts = lax.all_gather(parts, axes[k], axis=0, tiled=True)
    carried = [lax.axis_size(axes[k]) for k in reversed(sequence)]
    parts = parts.reshape(*carried, *array.shape)
    turned = sorted(range(len(sequence)), key=lambda place: sequence[len(sequence) - 1 - place])
    return parts.transpose(*turned, *range(len(sequence), parts.ndim)).reshape(-1, *array.shape)


def gather_axes(array, axes, sequence, dim):
    return joined_along(stacked_from(array, axes, sequence), dim)


def side_by_side(arrays, axis, dim, along):
    ends, at = ([], 0)
    for a in arrays[:-1]:
        at += a.shape[along]
        ends.append(at)
    both = jnp.concatenate(arrays, axis=along)
    return tuple(jnp.split(lax.all_gather(both, axis, axis=dim, tiled=True), ends, axis=along))


def copy_for_each(array, axis):
    copies = jnp.broadcast_to(array, (lax.axis_size(axis), *array.shape))
    return lax.all_to_all(copies, axis, split_axis=0, concat_axis=0, tiled=True)


def of_everyone(array, axis):
    return copy_for_each(array, axis).sum(axis=0)


def in_one(arrays, axis):
    ends = [0]
    for a in arrays:
        ends.append(ends[-1] + a.size)
    total = of_everyone(jnp.concatenate([a.ravel() for a in arrays]), axis)
    return tuple((total[b:e].reshape(a.shape) for a, b, e in zip(arrays, ends, ends[1:])))


def split_up(array, dim, peers):
    lengths = array.shape
    parts = array.reshape(*lengths[:dim], peers, lengths[dim] // peers, *lengths[dim + 1 :])
    return jnp.moveaxis(parts, dim, 0)


def summed_on_arrival(array, axis, dim):
    peers = lax.axis_size(axis)
    parts = lax.all_to_all(split_up(array, dim, peers), axis, 0, 0, tiled=True)
    return jnp.sum(parts.astype(jnp.float32), axis=0)


def sum_by_axis(array, axes, dim):
    far, near = axes
    parts = split_up(array, dim, lax.axis_size(far))
    nearer = summed_on_arrival(parts, near, dim + 1)
    arrived = lax.all_to_all(
        nearer.astype(jnp.bfloat16), far, split_axis=0, concat_axis=0, tiled=True
    )
    return arrived.astype(jnp.float32).sum(axis=0)


def over_axes(array, axes):
    return functools.reduce(lax.psum, axes, array)


def normalize(values):
    widened = values.astype(jnp.float32)
    radius = jnp.sqrt(jnp.sum(widened * widened, axis=-1, keepdims=True) + epsilon)
    return (widened / radius, radius)


def through_norm(grad_unit, unit, radius):
    inner = jnp.sum(unit * grad_unit, axis=-1, keepdims=True)
    return (grad_unit - unit * inner) / radius


def scores(left, right):
    return logit_scale * lax.dot_general(
        left, right, (((1,), (1,)), ((), ())), preferred_element_type=jnp.float32
    )


def contract_rows(weights_part, image_tile):
    return lax.dot_general(
        weights_part, image_tile, (((0,), (0,)), ((), ())), preferred_element_type=jnp.float32
    )


def pair_scores(image_tile, text_tile, audio_tile):
    text_scores = scores(image_tile, text_tile)
    audio_scores = scores(image_tile, audio_tile)
    return (
        text_scores,
        audio_scores,
        jnp.exp(text_scores - logit_scale),
        jnp.exp(audio_scores - logit_scale),
    )


def softmax_weights(exp_tile, row_total, column_total, twice_diagonal):
    return (
        exp_tile / row_total[:, None] + exp_tile / column_total[None, :] - twice_diagonal
    ).astype(jnp.bfloat16)


def own_logs(totals, first_row, amount):
    return jnp.sum(jnp.log(lax.dynamic_slice_in_dim(totals, first_row, amount, 0)))


def shards(image, text, audio):
    rows_here = image.shape[0]
    feature_width = image.shape[1]
    image_unit, image_radius = normalize(image)
    text_unit, text_radius = normalize(text)
    audio_unit, audio_radius = normalize(audio)
    image_half = image_unit.astype(jnp.bfloat16)
    text_half = text_unit.astype(jnp.bfloat16)
    audio_half = audio_unit.astype(jnp.bfloat16)
    row_place = lax.axis_index(ROW)
    col_place = lax.axis_index(COL)
    row_count = lax.axis_size(ROW)
    col_count = lax.axis_size(COL)
    image_tile = gather_axes(image_half, COL, (1, 0, 2), 0)
    text_tile, audio_tile = side_by_side((text_half, audio_half), ROW, 0, 1)
    image_local = jnp.arange(col_count * rows_here, dtype=jnp.int32)
    image_ids = (
        image_local // rows_here * row_count + row_place
    ) * rows_here + image_local % rows_here
    pair_local = jnp.arange(row_count * rows_here, dtype=jnp.int32)
    pair_ids = (
        pair_local // rows_here * col_count + col_place
    ) * rows_here + pair_local % rows_here
    text_scores, audio_scores, text_exp, audio_exp = pair_scores(image_tile, text_tile, audio_tile)
    text_row, audio_row = in_one((jnp.sum(text_exp, axis=1), jnp.sum(audio_exp, axis=1)), COL)
    text_column, audio_column = in_one((jnp.sum(text_exp, axis=0), jnp.sum(audio_exp, axis=0)), ROW)
    diagonal = image_ids[:, None] == pair_ids[None, :]
    twice_diagonal = jnp.where(diagonal, 2.0, 0.0).astype(jnp.float32)
    text_weights = softmax_weights(text_exp, text_row, text_column, twice_diagonal)
    audio_weights = softmax_weights(audio_exp, audio_row, audio_column, twice_diagonal)
    image_part = logit_scale * sum_by_axis(
        (
            jnp.dot(text_weights, text_tile, preferred_element_type=jnp.float32)
            + jnp.dot(audio_weights, audio_tile, preferred_element_type=jnp.float32)
        ).astype(jnp.bfloat16),
        (("col_0", "col_1"), "col_2"),
        0,
    )
    partial_value = jnp.concatenate(
        [contract_rows(text_weights, image_tile), contract_rows(audio_weights, image_tile)], axis=1
    )
    pair_part = logit_scale * summed_on_arrival(partial_value.astype(jnp.bfloat16), ROW, 0)
    image_first = col_place * rows_here
    pair_first = row_place * rows_here
    loss_part = (
        own_logs(text_row, image_first, rows_here)
        + own_logs(audio_row, image_first, rows_here)
        + own_logs(text_column, pair_first, rows_here)
        + own_logs(audio_column, pair_first, rows_here)
        - 2.0 * jnp.sum(jnp.where(diagonal, text_scores + audio_scores, 0.0))
    )
    batch_size = rows_here * row_count * col_count
    loss = over_axes(loss_part, ROW_COL) / (4.0 * batch_size) + logit_scale
    return (
        through_norm(image_part, image_unit, image_radius),
        through_norm(pair_part[:, :feature_width], text_unit, text_radius),
        through_norm(pair_part[:, feature_width:], audio_unit, audio_radius),
        loss,
    )


def solution(mesh):
    split = Mesh(mesh.devices.reshape(2, 2, 8, 2, 4), ("row_0", "row_1", "col_0", "col_1", "col_2"))
    placed = (P(COL_ROW, None), P(ROW_COL, None), P(ROW_COL, None))
    return jax.shard_map(
        shards,
        mesh=split,
        in_specs=placed,
        out_specs=(P(COL_ROW, None), P(ROW_COL, None), P(ROW_COL, None), P()),
        check_vma=False,
    )
```

profile of v0, /device:TPU:24, one launch (start us, length us, event | category | flops | bytes accessed | tf_op | source)
XLA Modules:
  0.0 305.4 jit_solution(18293533622989130421)
XLA Ops:
  9.1 6.5 %all-gather = bf16[64,1024]{1,0:T(8,128)(2,1)} all-gather(bf16[32,1024]{1,0:T(8,128)(2,1)S(1)} %fusion.46), channel_id=2, replica_groups=mesh['row_0'=2,'row_1'=2,'col_0'=8,'col_1'=2,'col_2'=4] {'col_1'}, dimensions={0}, use_global_device_ids=true | all-gather | bytes 196608 | tf_op jit(solution)/shard_map/all_gather | solution.py:25
  15.7 41.2 %all-gather.4.cloned.1.call-done = bf16[16,32,1024]{2,1,0:T(8,128)(2,1)} async-done(((bf16[2,32,1024]{2,1,0:T(8,128)(2,1)}), bf16[16,32,1024]{2,1,0:T(8,128)(2,1)}) %all-gather.4.cloned.1.call-update) | async-done | bytes 1048592 | tf_op jit(solution)/shard_map/all_gather | solution.py:25
  60.0 6.5 %all_gather.15 = bf16[128,2048]{1,0:T(8,128)(2,1)S(1)} all-gather(bf16[32,2048]{1,0:T(8,128)(2,1)S(1)} %pad_maximum_fusion.1), channel_id=1, replica_groups=mesh['row_0'=2,'row_1'=2,'col_0'=8,'col_1'=2,'col_2'=4] {'row_0','row_1'}, dimensions={0}, use_global_device_ids=true | all-gather | bytes 655360 | tf_op jit(solution)/shard_map/all_gather | solution.py:42
  66.5 41.4 %all-gather.6.cloned.1.call-done = bf16[64,32,1024]{2,1,0:T(8,128)(2,1)} async-done(((bf16[16,32,1024]{2,1,0:T(8,128)(2,1)}), bf16[64,32,1024]{2,1,0:T(8,128)(2,1)}) %all-gather.6.cloned.1.call-update) | async-done | bytes 4194320 | tf_op jit(solution)/shard_map/all_gather | solution.py:25
  107.9 2.6 copy.12
  112.1 2.4 fusion
  115.1 4.1 %all-to-all-start.1 = ((f32[4,1,256]{2,1,0:T(1,128)}), f32[4,1,256]{2,1,0:T(1,128)S(1)}, u32[]{:S(2)}, u32[]{:S(2)}) async-start(f32[4,1,256]{2,1,0:T(1,128)} %broadcast_in_dim.37), calls=%async_computation.1 | async-start | bytes 8192 | tf_op jit(solution)/shard_map/all_to_all | solution.py:47
  121.0 2.0 broadcast_in_dim.36
  123.0 12.0 %all-to-all-start = ((f32[64,1,4096]{2,1,0:T(1,128)}), f32[64,1,4096]{2,1,0:T(1,128)S(1)}, u32[]{:S(2)}, u32[]{:S(2)}) async-start(f32[64,1,4096]{2,1,0:T(1,128)} %broadcast_in_dim.36), calls=%async_computation | async-start | bytes 2097152 | tf_op jit(solution)/shard_map/all_to_all | solution.py:47
  135.0 28.0 %all-to-all-done = f32[64,1,4096]{2,1,0:T(1,128)S(1)} async-done(((f32[64,1,4096]{2,1,0:T(1,128)}), f32[64,1,4096]{2,1,0:T(1,128)S(1)}, u32[]{:S(2)}, u32[]{:S(2)}) %all-to-all-start) | async-done | bytes 1048608 | tf_op jit(solution)/shard_map/all_to_all | solution.py:47
  163.9 2.5 fusion.10
  167.9 2.4 copy.23
  170.3 4.8 %all-to-all-start.2 = ((bf16[4,16,32,1024]{3,2,1,0:T(8,128)(2,1)}), bf16[4,16,32,1024]{3,2,1,0:T(8,128)(2,1)}, u32[]{:S(2)}, u32[]{:S(2)}) async-start(bf16[4,16,32,1024]{3,2,1,0:T(8,128)(2,1)} %bitcast.27), calls=%async_computation.2 | async-start | bytes 8388608 | tf_op jit(solution)/shard_map/all_to_all | solution.py:70
  175.8 3.3 %convolution_convert_fusion.1 = bf16[4,32,1024]{2,1,0:T(8,128)(2,1)S(1)} fusion(bf16[4,32,2048]{2,1,0:T(8,128)(2,1)S(1)} %bitcast.31, bf16[2048,1024,1]{1,0,2:T(8,128)(2,1)} %bitcast.25), kind=kOutput, calls=%fused_computation.11 | convolution fusion | flops 537001984 | bytes 4980736 | tf_op jit(solution)/shard_map/dot_general | solution.py:106
  180.7 42.2 %all-to-all-done.2 = bf16[4,16,32,1024]{3,2,1,0:T(8,128)(2,1)} async-done(((bf16[4,16,32,1024]{3,2,1,0:T(8,128)(2,1)}), bf16[4,16,32,1024]{3,2,1,0:T(8,128)(2,1)}, u32[]{:S(2)}, u32[]{:S(2)}) %all-to-all-start.2) | async-done | bytes 4194336 | tf_op jit(solution)/shard_map/all_to_all | solution.py:70
  222.8 5.5 %all-to-all-start.4 = ((bf16[4,32,2048]{2,1,0:T(8,128)(2,1)}), bf16[4,32,2048]{2,1,0:T(8,128)(2,1)S(1)}, u32[]{:S(2)}, u32[]{:S(2)}) async-start(bf16[4,32,2048]{2,1,0:T(8,128)(2,1)} %pad_maximum_fusion), calls=%async_computation.4 | async-start | bytes 1048576 | tf_op jit(solution)/shard_map/all_to_all | solution.py:70
  228.3 4.4 %reduce_sum.192 = bf16[16,32,1024]{2,1,0:T(8,128)(2,1)} reduce(bf16[4,16,32,1024]{3,2,1,0:T(8,128)(2,1)} %all-to-all-done.2, bf16[]{:T(256)} %constant.102.clone.1), dimensions={0}, to_apply=%region_9.10 | reduce | flops 1572864 | bytes 5242882 | tf_op jit(solution)/shard_map/reduce_sum | solution.py:71
  232.7 2.7 all-to-all-done.4
  235.5 7.1 %all-to-all-start.3 = ((bf16[16,32,1024]{2,1,0:T(8,128)(2,1)}), bf16[16,32,1024]{2,1,0:T(8,128)(2,1)S(1)}, u32[]{:S(2)}, u32[]{:S(2)}) async-start(bf16[16,32,1024]{2,1,0:T(8,128)(2,1)} %reduce_sum.192), calls=%async_computation.3 | async-start | bytes 2097152 | tf_op jit(solution)/shard_map/all_to_all | solution.py:78
  248.5 5.5 %psum.35 = f32[]{:T(128)} all-reduce(f32[]{:T(128)S(6)} %sub.53), channel_id=1, replica_groups=mesh['row_0'=2,'row_1'=2,'col_0'=8,'col_1'=2,'col_2'=4] {'row_0'}, use_global_device_ids=true, to_apply=%region_20.21 | all-reduce | flops 1 | bytes 8 | tf_op jit(solution)/shard_map/psum | solution.py:85
  254.0 3.1 %psum.36 = f32[]{:T(128)} all-reduce(f32[]{:T(128)} %psum.35), channel_id=1, replica_groups=mesh['row_0'=2,'row_1'=2,'col_0'=8,'col_1'=2,'col_2'=4] {'row_1'}, use_global_device_ids=true, to_apply=%region_21.22 | all-reduce | flops 1 | bytes 8 | tf_op jit(solution)/shard_map/psum | solution.py:85
  257.0 20.9 %psum.37 = f32[]{:T(128)} all-reduce(f32[]{:T(128)} %psum.36), channel_id=1, replica_groups=mesh['row_0'=2,'row_1'=2,'col_0'=8,'col_1'=2,'col_2'=4] {'col_0'}, use_global_device_ids=true, to_apply=%region_22.23 | all-reduce | flops 1 | bytes 8 | tf_op jit(solution)/shard_map/psum | solution.py:85
  277.9 7.1 %psum.38 = f32[]{:T(128)} all-reduce(f32[]{:T(128)} %psum.37), channel_id=1, replica_groups=mesh['row_0'=2,'row_1'=2,'col_0'=8,'col_1'=2,'col_2'=4] {'col_1'}, use_global_device_ids=true, to_apply=%region_23.24 | all-reduce | flops 1 | bytes 8 | tf_op jit(solution)/shard_map/psum | solution.py:85
  285.0 9.5 %psum.39 = f32[]{:T(128)} all-reduce(f32[]{:T(128)} %psum.38), channel_id=1, replica_groups=mesh['row_0'=2,'row_1'=2,'col_0'=8,'col_1'=2,'col_2'=4] {'col_2'}, use_global_device_ids=true, to_apply=%region_24.25 | all-reduce | flops 1 | bytes 8 | tf_op jit(solution)/shard_map/psum | solution.py:85
  (54 shorter events, 18.5 us)
Async XLA Ops:
  7.2 49.8 %all-gather.4.cloned.1.call-start = ((), (), s32[]{:S(2)}) async-start(), calls=%async_computation.5 | async-start | bytes 1179648 | tf_op jit(solution)/shard_map/all_gather | solution.py:25
  15.7 92.2 %all-gather.6.cloned.1.call-start = ((), (), s32[]{:S(2)}) async-start(), calls=%async_computation.6 | async-start | bytes 5242880 | tf_op jit(solution)/shard_map/all_gather | solution.py:25
  66.5 45.6 %copy-start.2 = (bf16[128,2048]{1,0:T(8,128)(2,1)}, bf16[128,2048]{1,0:T(8,128)(2,1)S(1)}, u32[]{:S(2)}) copy-start(bf16[128,2048]{1,0:T(8,128)(2,1)S(1)} %all_gather.15) | copy-start | bytes 1572868
  110.5 4.0 %copy-start = (bf16[8,2,4,32,1024]{4,3,2,1,0:T(8,128)(2,1)}, bf16[8,2,4,32,1024]{4,3,2,1,0:T(8,128)(2,1)S(1)}, u32[]{:S(2)}) copy-start(bf16[8,2,4,32,1024]{4,3,2,1,0:T(8,128)(2,1)S(1)} %copy.12) | copy-start | bytes 12582916
  115.1 5.8 %all-to-all-start.1 = ((f32[4,1,256]{2,1,0:T(1,128)}), f32[4,1,256]{2,1,0:T(1,128)S(1)}, u32[]{:S(2)}, u32[]{:S(2)}) async-start(f32[4,1,256]{2,1,0:T(1,128)} %broadcast_in_dim.37), calls=%async_computation.1 | async-start | bytes 8192 | tf_op jit(solution)/shard_map/all_to_all | solution.py:47
  123.0 40.0 %all-to-all-start = ((f32[64,1,4096]{2,1,0:T(1,128)}), f32[64,1,4096]{2,1,0:T(1,128)S(1)}, u32[]{:S(2)}, u32[]{:S(2)}) async-start(f32[64,1,4096]{2,1,0:T(1,128)} %broadcast_in_dim.36), calls=%async_computation | async-start | bytes 2097152 | tf_op jit(solution)/shard_map/all_to_all | solution.py:47
  163.9 2.5 copy-start.3
  170.3 52.5 %all-to-all-start.2 = ((bf16[4,16,32,1024]{3,2,1,0:T(8,128)(2,1)}), bf16[4,16,32,1024]{3,2,1,0:T(8,128)(2,1)}, u32[]{:S(2)}, u32[]{:S(2)}) async-start(bf16[4,16,32,1024]{3,2,1,0:T(8,128)(2,1)} %bitcast.27), calls=%async_computation.2 | async-start | bytes 8388608 | tf_op jit(solution)/shard_map/all_to_all | solution.py:70
  175.2 3.9 %copy-start.1 = (bf16[8,2,4,32,1024]{4,3,2,1,0:T(8,128)(2,1)S(1)}, bf16[8,2,4,32,1024]{4,3,2,1,0:T(8,128)(2,1)}, u32[]{:S(2)}) copy-start(bf16[8,2,4,32,1024]{4,3,2,1,0:T(8,128)(2,1)} %copy-done) | copy-start | bytes 12582916
  222.8 12.6 %all-to-all-start.4 = ((bf16[4,32,2048]{2,1,0:T(8,128)(2,1)}), bf16[4,32,2048]{2,1,0:T(8,128)(2,1)S(1)}, u32[]{:S(2)}, u32[]{:S(2)}) async-start(bf16[4,32,2048]{2,1,0:T(8,128)(2,1)} %pad_maximum_fusion), calls=%async_computation.4 | async-start | bytes 1048576 | tf_op jit(solution)/shard_map/all_to_all | solution.py:70
  228.3 67.0 %copy-start.5 = (bf16[32,1024]{1,0:T(8,128)(2,1)S(1)}, bf16[32,1024]{1,0:T(8,128)(2,1)}, u32[]{:S(2)}) copy-start(bf16[32,1024]{1,0:T(8,128)(2,1)} %param.4) | copy-start | bytes 196612
  228.3 67.0 %copy-start.6 = (bf16[32,1024]{1,0:T(8,128)(2,1)S(1)}, bf16[32,1024]{1,0:T(8,128)(2,1)}, u32[]{:S(2)}) copy-start(bf16[32,1024]{1,0:T(8,128)(2,1)} %param.5) | copy-start | bytes 196612
  228.3 68.2 %copy-start.4 = (bf16[32,1024]{1,0:T(8,128)(2,1)S(1)}, bf16[32,1024]{1,0:T(8,128)(2,1)}, u32[]{:S(2)}) copy-start(bf16[32,1024]{1,0:T(8,128)(2,1)} %param.3) | copy-start | bytes 196612
  235.5 60.9 %all-to-all-start.3 = ((bf16[16,32,1024]{2,1,0:T(8,128)(2,1)}), bf16[16,32,1024]{2,1,0:T(8,128)(2,1)S(1)}, u32[]{:S(2)}, u32[]{:S(2)}) async-start(bf16[16,32,1024]{2,1,0:T(8,128)(2,1)} %reduce_sum.192), calls=%async_computation.3 | async-start | bytes 2097152 | tf_op jit(solution)/shard_map/all_to_all | solution.py:78
Sparse Core Ops, SparseCore 0:
  15.8 41.1 all-gather.3
  58.8 49.1 all-gather.5
where the time goes:
time: 306 us; the launch traced here: 305 us
  waiting for transfers between devices  157 us (51%)
  blocking collectives  59.1 us (19%)
  starting transfers between devices  33.5 us (11%)
  between operations  19.3 us (6%)
  other arithmetic  16.6 us (5%)
  matrix products  11.9 us (4%)
  local copies, waits for them, and re-layouts  7.67 us (3%)
    all_gather x2, waiting for transfers between devices, stacked_from(): parts = lax.all_gather(parts, axes[k], axis=0, tiled=True)  82.7 us
    psum x5, blocking collectives, over_axes(): return functools.reduce(lax.psum, axes, array)  46 us
    all_to_all x2, waiting for transfers between devices, summed_on_arrival(): parts = lax.all_to_all(split_up(array, dim, peers), axis, 0, 0, tiled=True)  44.9 us
    all_to_all x2, waiting for transfers between devices, copy_for_each(): return lax.all_to_all(copies, axis, split_axis=0, concat_axis=0, tiled=True)  29.7 us
    all_to_all x2, starting transfers between devices, copy_for_each(): return lax.all_to_all(copies, axis, split_axis=0, concat_axis=0, tiled=True)  16.1 us
    all_to_all x2, starting transfers between devices, summed_on_arrival(): parts = lax.all_to_all(split_up(array, dim, peers), axis, 0, 0, tiled=True)  10.3 us
    all_to_all x1, starting transfers between devices, sum_by_axis(): lax.all_to_all(nearer.astype(jnp.bfloat16), far, split_axis=0, concat_axi...  7.08 us
    all_gather x1, blocking collectives, stacked_from(): parts = lax.all_gather(parts, axes[k], axis=0, tiled=True)  6.54 us
  transfers between devices with their start and end apart: 7, of which 6 were waited for; matrix products, arithmetic and copies ran while one was open for 5% of the time, Pallas kernels for 0%

commit v1 on v0

--- a/solution.py
+++ b/solution.py
@@ -22,7 +22,9 @@
 def stacked_from(array, axes, sequence):
     parts = array[None]
     for k in sequence:
-        parts = lax.all_gather(parts, axes[k], axis=0, tiled=True)
+        parts = jnp.concatenate(
+            lax.all_to_all(jnp.stack([parts] * lax.axis_size(axes[k])), axes[k], 0, 0), axis=0
+        )
     carried = [lax.axis_size(axes[k]) for k in reversed(sequence)]
     parts = parts.reshape(*carried, *array.shape)
     turned = sorted(range(len(sequence)), key=lambda place: sequence[len(sequence) - 1 - place])

time: 306 us -> 286 us (0.935)
  waiting for transfers between devices: 157 us -> 114 us
  blocking collectives: 59.1 us -> 95.5 us
  between operations: 19.3 us -> 5.91 us
    all_gather x2 -> x0, waiting for transfers between devices: 82.7 us -> none  [stacked_from(): parts = lax.all_gather(parts, axes[k], axis=0, tiled=True)]
    all_to_all x0 -> x2, blocking collectives: none -> 42.9 us  [stacked_from(): lax.all_to_all(jnp.stack([parts] * lax.axis_size(axes[k])), axes[k], 0, 0)]
    all_to_all x0 -> x1, waiting for transfers between devices: none -> 39.1 us  [stacked_from(): lax.all_to_all(jnp.stack([parts] * lax.axis_size(axes[k])), axes[k], 0, 0)]
    all_gather x1 -> x0, blocking collectives: 6.54 us -> none  [stacked_from(): parts = lax.all_gather(parts, axes[k], axis=0, tiled=True)]
    another operation x0 -> x3, local copies, waits for them, and re-layouts: none -> 5.33 us  [the longest x2 2.7 us: stacked_from(): jnp.stack([parts] * lax.axis_size(axes[k]))]
    all_to_all x0 -> x1, starting transfers between devices: none -> 4.99 us  [stacked_from(): lax.all_to_all(jnp.stack([parts] * lax.axis_size(axes[k])), axes[k], 0, 0)]
    all_to_all x2, starting transfers between devices: 16.1 us -> 12.3 us  [copy_for_each(): return lax.all_to_all(copies, axis, split_axis=0, concat_axis=0, tiled=True)]
  transfers between devices with their start and end apart: 7 -> 6, of which waited for: 6 -> 5; matrix products, arithmetic and copies ran while one was open for 5% -> 5% of each run, Pallas kernels for 0% -> 0%
where the time goes in v1:
time: 286 us; the launch traced here: 285 us
  waiting for transfers between devices  114 us (40%)
  blocking collectives  95.5 us (33%)
  starting transfers between devices  34.1 us (12%)
  other arithmetic  14.1 us (5%)
  matrix products  11.9 us (4%)
  local copies, waits for them, and re-layouts  10.4 us (4%)
  between operations  5.91 us (2%)
    psum x5, blocking collectives, over_axes(): return functools.reduce(lax.psum, axes, array)  46.1 us
    all_to_all x2, waiting for transfers between devices, summed_on_arrival(): parts = lax.all_to_all(split_up(array, dim, peers), axis, 0, 0, tiled=True)  44.7 us
    all_to_all x2, blocking collectives, stacked_from(): lax.all_to_all(jnp.stack([parts] * lax.axis_size(axes[k])), axes[k], 0, 0)  42.9 us
    all_to_all x1, waiting for transfers between devices, stacked_from(): lax.all_to_all(jnp.stack([parts] * lax.axis_size(axes[k])), axes[k], 0, 0)  39.1 us
    all_to_all x2, waiting for transfers between devices, copy_for_each(): return lax.all_to_all(copies, axis, split_axis=0, concat_axis=0, tiled=True)  29.7 us
    all_to_all x2, starting transfers between devices, copy_for_each(): return lax.all_to_all(copies, axis, split_axis=0, concat_axis=0, tiled=True)  12.3 us
    all_to_all x2, starting transfers between devices, summed_on_arrival(): parts = lax.all_to_all(split_up(array, dim, peers), axis, 0, 0, tiled=True)  9.69 us
    all_to_all x1, starting transfers between devices, sum_by_axis(): lax.all_to_all(nearer.astype(jnp.bfloat16), far, split_axis=0, concat_axi...  7.07 us
  transfers between devices with their start and end apart: 6, of which 5 were waited for; matrix products, arithmetic and copies ran while one was open for 5% of the time, Pallas kernels for 0%

profile of v1, /device:TPU:24, one launch (start us, length us, event | category | flops | bytes accessed | tf_op | source)
XLA Modules:
  0.0 285.4 jit_solution(13658419012430485261)
XLA Ops:
  2.6 7.0 %all_to_all.42 = bf16[2,1,32,1024]{3,2,1,0:T(8,128)(2,1)S(1)} all-to-all(bf16[2,1,32,1024]{3,2,1,0:T(8,128)(2,1)S(1)} %pad_maximum_fusion.1), channel_id=1, replica_groups=mesh['row_0'=2,'row_1'=2,'col_0'=8,'col_1'=2,'col_2'=4] {'col_1'}, dimensions={0} | all-to-all | bytes 262144 | tf_op jit(solution)/shard_map/all_to_all | solution.py:26
  9.7 35.8 %all_to_all.43 = bf16[8,2,32,1024]{3,2,1,0:T(8,128)(2,1)S(1)} all-to-all(bf16[8,2,32,1024]{3,2,1,0:T(8,128)(2,1)S(1)} %stack.10), channel_id=1, replica_groups=mesh['row_0'=2,'row_1'=2,'col_0'=8,'col_1'=2,'col_2'=4] {'col_0'}, dimensions={0} | all-to-all | bytes 2097152 | tf_op jit(solution)/shard_map/all_to_all | solution.py:26
  45.6 2.6 stack.11
  48.2 5.0 %all-to-all-start.2 = ((bf16[4,16,32,1024]{3,2,1,0:T(8,128)(2,1)}), bf16[4,16,32,1024]{3,2,1,0:T(8,128)(2,1)}, u32[]{:S(2)}, u32[]{:S(2)}) async-start(bf16[4,16,32,1024]{3,2,1,0:T(8,128)(2,1)} %stack.11), calls=%async_computation.2 | async-start | bytes 8388608 | tf_op jit(solution)/shard_map/all_to_all | solution.py:26
  53.6 6.5 %all_gather.3 = bf16[128,2048]{1,0:T(8,128)(2,1)S(1)} all-gather(bf16[32,2048]{1,0:T(8,128)(2,1)S(1)} %pad_maximum_fusion.2), channel_id=1, replica_groups=mesh['row_0'=2,'row_1'=2,'col_0'=8,'col_1'=2,'col_2'=4] {'row_0','row_1'}, dimensions={0}, use_global_device_ids=true | all-gather | bytes 655360 | tf_op jit(solution)/shard_map/all_gather | solution.py:44
  60.1 39.1 %all-to-all-done.2 = bf16[4,16,32,1024]{3,2,1,0:T(8,128)(2,1)} async-done(((bf16[4,16,32,1024]{3,2,1,0:T(8,128)(2,1)}), bf16[4,16,32,1024]{3,2,1,0:T(8,128)(2,1)}, u32[]{:S(2)}, u32[]{:S(2)}) %all-to-all-start.2) | async-done | bytes 4194336 | tf_op jit(solution)/shard_map/all_to_all | solution.py:26
  99.2 2.6 copy.11
  103.4 2.4 fusion
  106.4 4.0 %all-to-all-start.4 = ((f32[4,1,256]{2,1,0:T(1,128)}), f32[4,1,256]{2,1,0:T(1,128)S(1)}, u32[]{:S(2)}, u32[]{:S(2)}) async-start(f32[4,1,256]{2,1,0:T(1,128)} %broadcast_in_dim.19), calls=%async_computation.4 | async-start | bytes 8192 | tf_op jit(solution)/shard_map/all_to_all | solution.py:49
  114.1 8.4 %all-to-all-start.3 = ((f32[64,1,4096]{2,1,0:T(1,128)}), f32[64,1,4096]{2,1,0:T(1,128)S(1)}, u32[]{:S(2)}, u32[]{:S(2)}) async-start(f32[64,1,4096]{2,1,0:T(1,128)} %broadcast_in_dim.18), calls=%async_computation.3 | async-start | bytes 2097152 | tf_op jit(solution)/shard_map/all_to_all | solution.py:49
  122.6 28.0 %all-to-all-done.3 = f32[64,1,4096]{2,1,0:T(1,128)S(1)} async-done(((f32[64,1,4096]{2,1,0:T(1,128)}), f32[64,1,4096]{2,1,0:T(1,128)S(1)}, u32[]{:S(2)}, u32[]{:S(2)}) %all-to-all-start.3) | async-done | bytes 1048608 | tf_op jit(solution)/shard_map/all_to_all | solution.py:49
  151.4 2.5 fusion.10
  157.8 5.0 %all-to-all-start.5 = ((bf16[4,16,32,1024]{3,2,1,0:T(8,128)(2,1)}), bf16[4,16,32,1024]{3,2,1,0:T(8,128)(2,1)}, u32[]{:S(2)}, u32[]{:S(2)}) async-start(bf16[4,16,32,1024]{3,2,1,0:T(8,128)(2,1)} %bitcast.30), calls=%async_computation.5 | async-start | bytes 8388608 | tf_op jit(solution)/shard_map/all_to_all | solution.py:72
  163.5 3.3 %convolution_convert_fusion.1 = bf16[4,32,1024]{2,1,0:T(8,128)(2,1)S(1)} fusion(bf16[4,32,2048]{2,1,0:T(8,128)(2,1)S(1)} %bitcast.34, bf16[2048,1024,1]{1,0,2:T(8,128)(2,1)} %bitcast.28), kind=kOutput, calls=%fused_computation.11 | convolution fusion | flops 537001984 | bytes 4980736 | tf_op jit(solution)/shard_map/dot_general | solution.py:108
  168.4 42.0 %all-to-all-done.5 = bf16[4,16,32,1024]{3,2,1,0:T(8,128)(2,1)} async-done(((bf16[4,16,32,1024]{3,2,1,0:T(8,128)(2,1)}), bf16[4,16,32,1024]{3,2,1,0:T(8,128)(2,1)}, u32[]{:S(2)}, u32[]{:S(2)}) %all-to-all-start.5) | async-done | bytes 4194336 | tf_op jit(solution)/shard_map/all_to_all | solution.py:72
  210.4 4.7 %all-to-all-start.7 = ((bf16[4,32,2048]{2,1,0:T(8,128)(2,1)}), bf16[4,32,2048]{2,1,0:T(8,128)(2,1)S(1)}, u32[]{:S(2)}, u32[]{:S(2)}) async-start(bf16[4,32,2048]{2,1,0:T(8,128)(2,1)} %pad_maximum_fusion), calls=%async_computation.7 | async-start | bytes 1048576 | tf_op jit(solution)/shard_map/all_to_all | solution.py:72
  215.0 4.4 %reduce_sum.192 = bf16[16,32,1024]{2,1,0:T(8,128)(2,1)} reduce(bf16[4,16,32,1024]{3,2,1,0:T(8,128)(2,1)} %all-to-all-done.5, bf16[]{:T(256)} %constant.102.clone.1), dimensions={0}, to_apply=%region_9.10 | reduce | flops 1572864 | bytes 5242882 | tf_op jit(solution)/shard_map/reduce_sum | solution.py:73
  219.5 2.8 all-to-all-done.7
  222.2 7.1 %all-to-all-start.6 = ((bf16[16,32,1024]{2,1,0:T(8,128)(2,1)}), bf16[16,32,1024]{2,1,0:T(8,128)(2,1)S(1)}, u32[]{:S(2)}, u32[]{:S(2)}) async-start(bf16[16,32,1024]{2,1,0:T(8,128)(2,1)} %reduce_sum.192), calls=%async_computation.6 | async-start | bytes 2097152 | tf_op jit(solution)/shard_map/all_to_all | solution.py:80
  235.2 5.5 %psum.35 = f32[]{:T(128)} all-reduce(f32[]{:T(128)S(6)} %sub.53), channel_id=1, replica_groups=mesh['row_0'=2,'row_1'=2,'col_0'=8,'col_1'=2,'col_2'=4] {'row_0'}, use_global_device_ids=true, to_apply=%region_20.21 | all-reduce | flops 1 | bytes 8 | tf_op jit(solution)/shard_map/psum | solution.py:87
  240.7 3.1 %psum.36 = f32[]{:T(128)} all-reduce(f32[]{:T(128)} %psum.35), channel_id=1, replica_groups=mesh['row_0'=2,'row_1'=2,'col_0'=8,'col_1'=2,'col_2'=4] {'row_1'}, use_global_device_ids=true, to_apply=%region_21.22 | all-reduce | flops 1 | bytes 8 | tf_op jit(solution)/shard_map/psum | solution.py:87
  243.8 20.9 %psum.37 = f32[]{:T(128)} all-reduce(f32[]{:T(128)} %psum.36), channel_id=1, replica_groups=mesh['row_0'=2,'row_1'=2,'col_0'=8,'col_1'=2,'col_2'=4] {'col_0'}, use_global_device_ids=true, to_apply=%region_22.23 | all-reduce | flops 1 | bytes 8 | tf_op jit(solution)/shard_map/psum | solution.py:87
  264.7 7.1 %psum.38 = f32[]{:T(128)} all-reduce(f32[]{:T(128)} %psum.37), channel_id=1, replica_groups=mesh['row_0'=2,'row_1'=2,'col_0'=8,'col_1'=2,'col_2'=4] {'col_1'}, use_global_device_ids=true, to_apply=%region_23.24 | all-reduce | flops 1 | bytes 8 | tf_op jit(solution)/shard_map/psum | solution.py:87
  271.7 9.6 %psum.39 = f32[]{:T(128)} all-reduce(f32[]{:T(128)} %psum.38), channel_id=1, replica_groups=mesh['row_0'=2,'row_1'=2,'col_0'=8,'col_1'=2,'col_2'=4] {'col_2'}, use_global_device_ids=true, to_apply=%region_24.25 | all-reduce | flops 1 | bytes 8 | tf_op jit(solution)/shard_map/psum | solution.py:87
  (54 shorter events, 20.3 us)
Async XLA Ops:
  48.2 5.0 %copy-start.5 = (bf16[32,1024]{1,0:T(8,128)(2,1)S(1)}, bf16[32,1024]{1,0:T(8,128)(2,1)}, u32[]{:S(2)}) copy-start(bf16[32,1024]{1,0:T(8,128)(2,1)} %param.4) | copy-start | bytes 196612
  48.2 5.2 %copy-start.6 = (bf16[32,1024]{1,0:T(8,128)(2,1)S(1)}, bf16[32,1024]{1,0:T(8,128)(2,1)}, u32[]{:S(2)}) copy-start(bf16[32,1024]{1,0:T(8,128)(2,1)} %param.5) | copy-start | bytes 196612
  48.2 51.0 %all-to-all-start.2 = ((bf16[4,16,32,1024]{3,2,1,0:T(8,128)(2,1)}), bf16[4,16,32,1024]{3,2,1,0:T(8,128)(2,1)}, u32[]{:S(2)}, u32[]{:S(2)}) async-start(bf16[4,16,32,1024]{3,2,1,0:T(8,128)(2,1)} %stack.11), calls=%async_computation.2 | async-start | bytes 8388608 | tf_op jit(solution)/shard_map/all_to_all | solution.py:26
  60.1 43.2 %copy-start.2 = (bf16[128,2048]{1,0:T(8,128)(2,1)}, bf16[128,2048]{1,0:T(8,128)(2,1)S(1)}, u32[]{:S(2)}) copy-start(bf16[128,2048]{1,0:T(8,128)(2,1)S(1)} %all_gather.3) | copy-start | bytes 1572868
  101.8 4.0 %copy-start = (bf16[4,8,2,32,1024]{4,3,0,2,1:T(8,128)(2,1)}, bf16[4,8,2,32,1024]{4,3,0,2,1:T(8,128)(2,1)S(1)}, u32[]{:S(2)}) copy-start(bf16[4,8,2,32,1024]{4,3,0,2,1:T(8,128)(2,1)S(1)} %copy.11) | copy-start | bytes 12582916
  106.4 5.8 %all-to-all-start.4 = ((f32[4,1,256]{2,1,0:T(1,128)}), f32[4,1,256]{2,1,0:T(1,128)S(1)}, u32[]{:S(2)}, u32[]{:S(2)}) async-start(f32[4,1,256]{2,1,0:T(1,128)} %broadcast_in_dim.19), calls=%async_computation.4 | async-start | bytes 8192 | tf_op jit(solution)/shard_map/all_to_all | solution.py:49
  114.1 36.4 %all-to-all-start.3 = ((f32[64,1,4096]{2,1,0:T(1,128)}), f32[64,1,4096]{2,1,0:T(1,128)S(1)}, u32[]{:S(2)}, u32[]{:S(2)}) async-start(f32[64,1,4096]{2,1,0:T(1,128)} %broadcast_in_dim.18), calls=%async_computation.3 | async-start | bytes 2097152 | tf_op jit(solution)/shard_map/all_to_all | solution.py:49
  151.4 2.5 copy-start.3
  157.8 52.5 %all-to-all-start.5 = ((bf16[4,16,32,1024]{3,2,1,0:T(8,128)(2,1)}), bf16[4,16,32,1024]{3,2,1,0:T(8,128)(2,1)}, u32[]{:S(2)}, u32[]{:S(2)}) async-start(bf16[4,16,32,1024]{3,2,1,0:T(8,128)(2,1)} %bitcast.30), calls=%async_computation.5 | async-start | bytes 8388608 | tf_op jit(solution)/shard_map/all_to_all | solution.py:72
  162.9 3.9 %copy-start.1 = (bf16[4,8,2,32,1024]{4,3,0,2,1:T(8,128)(2,1)S(1)}, bf16[4,8,2,32,1024]{4,3,0,2,1:T(8,128)(2,1)}, u32[]{:S(2)}) copy-start(bf16[4,8,2,32,1024]{4,3,0,2,1:T(8,128)(2,1)} %copy-done) | copy-start | bytes 12582916
  210.4 11.9 %all-to-all-start.7 = ((bf16[4,32,2048]{2,1,0:T(8,128)(2,1)}), bf16[4,32,2048]{2,1,0:T(8,128)(2,1)S(1)}, u32[]{:S(2)}, u32[]{:S(2)}) async-start(bf16[4,32,2048]{2,1,0:T(8,128)(2,1)} %pad_maximum_fusion), calls=%async_computation.7 | async-start | bytes 1048576 | tf_op jit(solution)/shard_map/all_to_all | solution.py:72
  215.0 68.3 %copy-start.4 = (bf16[32,1024]{1,0:T(8,128)(2,1)S(1)}, bf16[32,1024]{1,0:T(8,128)(2,1)}, u32[]{:S(2)}) copy-start(bf16[32,1024]{1,0:T(8,128)(2,1)} %param.3) | copy-start | bytes 196612
  222.2 60.9 %all-to-all-start.6 = ((bf16[16,32,1024]{2,1,0:T(8,128)(2,1)}), bf16[16,32,1024]{2,1,0:T(8,128)(2,1)S(1)}, u32[]{:S(2)}, u32[]{:S(2)}) async-start(bf16[16,32,1024]{2,1,0:T(8,128)(2,1)} %reduce_sum.192), calls=%async_computation.6 | async-start | bytes 2097152 | tf_op jit(solution)/shard_map/all_to_all | solution.py:80
